TPU v7x, 32 devices: a whole 2x2x4 slice. The times are simulated.
32 devices in a mesh: groups: 2 (over y), expert: 4 (over z), dp: 2 (over core), tensor: 2 (over x).
Axes of the slice: x: 2, y: 2, z: 4, core: 2. Of those that a mesh axis runs over, the one named last changes fastest.
Arguments:
- tokens: bfloat16 [2, 2048, 2048], P('dp', ('groups', 'expert', 'tensor')), parts along dimension 1, may hold values from -6 to 6
- proj_weight: bfloat16 [4, 2048, 3584], P('expert', 'dp', 'tensor'), may hold values from -0.125 to 0.125
- slot_grads: bfloat16 [2, 4, 32, 3584], P('dp', 'expert', 'groups', 'tensor'), parts along dimension 2, may hold values from -1.5 to 1.5
- gate_weights: float32 [2, 2, 32], P('dp', None, 'groups'), parts along dimension 2, may hold values from 0.2 to 1
- selected: int32 [2, 2, 32], P('dp', None, 'groups'), parts along dimension 2, may hold values from 0 to 1023, as said below
Outputs:
- token_grads: bfloat16 [2, 2048, 2048], P('dp', ('groups', 'expert', 'tensor')), parts along dimension 1
- weight_grads: bfloat16 [8, 2048, 3584], P(('groups', 'expert'), 'dp', 'tensor'), parts along dimension 0
There are 2 independent parts, one for each index of `groups`. A program takes and returns all parts, laid end to end along the dimension named above; an argument that names none is the same for every part. Nothing has to cross between parts.
Inputs may be any that keep to these rules, and one draw needn't show every extreme that they name: `selected`: each entry names a token of its own group. Within one group and one expert the 16 entries are distinct. In each group an expert takes at most 4 tokens from the 128 tokens of one device (tokens k * 128 to (k + 1) * 128 - 1), and exactly 4 from some devices.
All inputs are finite; a program needn't handle non-finite values.
Results may differ from a plain program's by a relative error of at most 0.011.
Values may be sent and summed in bfloat16 or wider, within the bound.
No kernel may reach another device: no remote copies, remote signals or barrier semaphores. Data moves between devices by JAX's collectives and lax.ppermute only.
A program may use at most 64 MiB of HBM per device.

v0:
```python
import jax
import jax.numpy as jnp
from jax import lax
from jax.sharding import PartitionSpec as P

MOST = 4


def local(tokens, proj_weight, slot_grads, gate_weights, selected):
    n_tensor = lax.axis_size("tensor")
    n_expert = lax.axis_size("expert")
    n_data = lax.axis_size("dp")
    owners = n_expert * n_tensor
    own_expert = lax.axis_index("expert")
    own_owner = own_expert * n_tensor + lax.axis_index("tensor")
    token_rows = tokens[0]
    tok_dev = token_rows.shape[0]
    features = token_rows.shape[1]
    chosen = selected[0]
    experts = chosen.shape[0]
    capacity = chosen.shape[1]
    owner_of = chosen // tok_dev
    local_row = chosen % tok_dev
    slot_ids = jnp.arange(capacity)
    earlier = slot_ids[None, :] < slot_ids[:, None]
    same_owner = owner_of[:, :, None] == owner_of[:, None, :]
    arrival = jnp.sum(same_owner & earlier[None], axis=2)
    slot_pos = jnp.arange(MOST)
    local_hits = owner_of == own_owner
    selector = local_hits[:, None, :] & (arrival[:, None, :] == slot_pos[None, :, None])
    filled = jnp.any(selector, axis=2)
    send_row = jnp.sum(jnp.where(selector, local_row[:, None, :], 0), axis=2)
    outgoing = jnp.where(filled[..., None], token_rows[send_row], jnp.zeros((), jnp.bfloat16))
    outgoing_all = jnp.broadcast_to(outgoing[:, None, None], (experts, 2, n_tensor, MOST, features))
    incoming = lax.all_to_all(
        outgoing_all.reshape(owners, MOST, features),
        ("expert", "tensor"),
        split_axis=0,
        concat_axis=0,
        tiled=True,
    )
    incoming = incoming.reshape(owners * MOST, features)
    own_index = own_expert // 2
    own_owners = lax.dynamic_index_in_dim(owner_of, own_index, 0, keepdims=False)
    own_arrival = lax.dynamic_index_in_dim(arrival, own_index, 0, keepdims=False)
    slot_rows = incoming[own_owners * MOST + own_arrival]
    gate_row = lax.dynamic_index_in_dim(gate_weights[0], own_index, 0, keepdims=False)
    scaled = (gate_row[:, None] * slot_grads[0, 0].astype(jnp.float32)).astype(jnp.bfloat16)
    partial_value_sum = lax.dot_general(
        scaled,
        lax.all_gather(proj_weight, "dp", axis=1, tiled=True)[0],
        (((1,), (1,)), ((), ())),
        preferred_element_type=jnp.float32,
    ).astype(jnp.bfloat16)
    slot_equal_mask = (own_owners[None, None, :] == jnp.arange(owners)[:, None, None]) & (
        own_arrival[None, None, :] == slot_pos[None, :, None]
    )
    slot_used = jnp.any(slot_equal_mask, axis=2)
    slot_index = jnp.sum(jnp.where(slot_equal_mask, slot_ids[None, None, :], 0), axis=2)
    returning = jnp.where(
        slot_used[..., None], partial_value_sum[slot_index], jnp.zeros((), jnp.bfloat16)
    )
    arrived = lax.all_to_all(
        returning, ("expert", "tensor"), split_axis=0, concat_axis=0, tiled=True
    )
    arrived = arrived.reshape(owners * MOST, features)
    complete_row = jnp.broadcast_to(send_row[:, None, None], (experts, 2, n_tensor, MOST)).reshape(
        owners * MOST
    )
    used_full = jnp.broadcast_to(filled[:, None, None], (experts, 2, n_tensor, MOST)).reshape(
        owners * MOST
    )
    placement = (jnp.arange(tok_dev)[:, None] == complete_row[None, :]) & used_full[None, :]
    token_grads = jnp.dot(
        placement.astype(jnp.bfloat16), arrived, preferred_element_type=jnp.float32
    )
    token_grads = token_grads.astype(jnp.bfloat16)[None]
    column_share = lax.all_to_all(slot_rows, "dp", split_axis=1, concat_axis=0, tiled=True)
    scaled_all = lax.all_gather(scaled, "dp", axis=0, tiled=True)
    column_share = column_share.reshape(n_data, capacity, column_share.shape[1])
    scaled_all = scaled_all.reshape(n_data, capacity, scaled_all.shape[1])
    per_group = jnp.einsum(
        "gcd,gcf->gdf", column_share, scaled_all, preferred_element_type=jnp.float32
    )
    per_group = per_group.astype(jnp.bfloat16).astype(jnp.float32)
    weight_grads = jnp.sum(per_group, axis=0).astype(jnp.bfloat16)[None]
    return (token_grads, weight_grads)


def solution(mesh):
    in_specs = (
        P("dp", ("groups", "expert", "tensor"), None),
        P("expert", "dp", "tensor"),
        P("dp", "expert", "groups", "tensor"),
        P("dp", None, "groups"),
        P("dp", None, "groups"),
    )
    out_specs = (
        P("dp", ("groups", "expert", "tensor"), None),
        P(("groups", "expert"), "dp", "tensor"),
    )
    return jax.shard_map(local, mesh=mesh, in_specs=in_specs, out_specs=out_specs, check_vma=False)
```

profile of v0, /device:TPU:0, one launch (start us, length us, event | category | flops | bytes accessed | tf_op | source)
XLA Modules:
  0.0 58.4 jit_solution(3440165395489555670)
XLA Ops:
  7.2 0.0 copy-start
  7.2 0.0 all-gather.2.cloned.1.call-start
  7.2 0.7 %all-gather.2.cloned.1.call-update = ((bf16[1,1024,1792]{2,1,0:T(8,128)(2,1)}), bf16[1,2048,1792]{2,1,0:T(8,128)(2,1)}) async-update(((), (), s32[]{:S(2)}) %all-gather.2.cloned.1.call-start, bf16[1,1024,1792]{2,1,0:T(8,128)(2,1)} %param.6) | async-update | bytes 14680088
  7.9 0.7 %broadcast_compare_fusion = (pred[2,16]{1,0:T(4,128)(4,1)S(1)}, s32[2,16]{1,0:T(2,128)S(1)}) fusion(s32[]{:T(128)S(6)} %add.79, s32[1,2,16]{2,1,0:T(2,128)} %param.9), kind=kLoop, calls=%fused_computation.53 | loop fusion | flops 512 | bytes 292 | tf_op jit(solution)/shard_map/eq | solution.py:29
  8.6 0.2 convert_reduce_fusion.1
  8.8 0.7 %and_select_fusion.1 = s32[2,16]{1,0:T(2,128)S(1)} fusion(s32[1,2,16]{2,1,0:T(2,128)} %param.9), kind=kLoop, calls=%fused_computation.41 | loop fusion | flops 352 | bytes 256 | tf_op jit(solution)/shard_map/jit(remainder)/select_n | solution.py:23
  9.5 0.1 select_reduce_fusion
  9.7 0.1 reshape.265
  9.7 0.0 copy-done
  9.8 0.6 gather_fusion.1
  10.4 0.2 fusion.19
  10.5 0.1 broadcast_select_fusion.1
  10.6 0.7 %broadcast_in_dim.104 = bf16[2,2,2,4,2048]{4,3,2,1,0:T(4,128)(2,1)} broadcast(bf16[2,4,2048]{2,1,0:T(4,128)(2,1)S(1)} %broadcast_select_fusion.1), dimensions={0,3,4} | broadcast | bytes 163840 | tf_op jit(solution)/shard_map/broadcast_in_dim | solution.py:34
  11.3 7.3 %all-to-all-start.1 = ((bf16[8,4,2048]{2,1,0:T(4,128)(2,1)}), bf16[8,4,2048]{2,1,0:T(4,128)(2,1)S(1)}, u32[]{:S(2)}, u32[]{:S(2)}) async-start(bf16[8,4,2048]{2,1,0:T(4,128)(2,1)} %bitcast.10), calls=%async_computation.1 | async-start | bytes 262144 | tf_op jit(solution)/shard_map/all_to_all | solution.py:35
  18.6 0.7 %fusion.20 = f32[16]{0:T(128)S(1)} fusion(f32[1,2,16]{2,1,0:T(2,128)} %param.8, s32[]{:T(128)S(6)} %select_n.92), kind=kLoop, calls=%fused_computation.51 | loop fusion | bytes 132 | tf_op jit(solution)/shard_map/jit(dynamic_index_in_dim)/dynamic_slice | solution.py:47
  19.3 0.2 and_reduce_fusion
  19.5 0.2 fusion.17
  19.6 0.9 %fusion.8 = bf16[16,1792]{1,0:T(8,128)(2,1)S(1)} fusion(bf16[1,1,16,1792]{3,2,1,0:T(8,128)(2,1)} %param.7, f32[16]{0:T(128)S(1)} %fusion.20), kind=kLoop, calls=%fused_computation.14 | loop fusion | flops 86016 | bytes 114752 | tf_op jit(solution)/shard_map/convert_element_type | solution.py:48
  20.5 0.1 copy.10
  20.6 0.1 copy.11
  20.7 0.1 reshape.257
  20.8 0.1 and.91
  20.9 0.1 eq.100
  21.0 4.9 %all-to-all-done.1 = bf16[8,4,2048]{2,1,0:T(4,128)(2,1)S(1)} async-done(((bf16[8,4,2048]{2,1,0:T(4,128)(2,1)}), bf16[8,4,2048]{2,1,0:T(4,128)(2,1)S(1)}, u32[]{:S(2)}, u32[]{:S(2)}) %all-to-all-start.1) | async-done | bytes 131104 | tf_op jit(solution)/shard_map/all_to_all | solution.py:35
  26.0 0.6 %gather_fusion.2 = bf16[16,2048]{1,0:T(8,128)(2,1)S(1)} fusion(bf16[32,2048]{1,0:T(8,128)(2,1)S(1)} %reshape.252, s32[1024]{0:T(1024)S(1)} %pad_clamp_fusion), kind=kCustom, calls=%fused_computation.2 | custom fusion | bytes 131136 | tf_op jit(solution)/shard_map/gather | solution.py:46
  26.6 0.6 %copy.15 = bf16[2,2,8,1024]{3,2,0,1:T(8,128)(2,1)} copy(bf16[2,2,8,1024]{3,2,1,0:T(8,128)(2,1)S(1)} %bitcast.71) | data formatting | bytes 131072 | tf_op jit(solution)/shard_map/all_to_all | solution.py:78
  27.2 3.3 %all-to-all-start.2 = ((bf16[16,2,1024]{2,0,1:T(8,128)(2,1)}), bf16[16,2,1024]{2,0,1:T(8,128)(2,1)S(1)}, u32[]{:S(2)}, u32[]{:S(2)}) async-start(bf16[16,2,1024]{2,0,1:T(8,128)(2,1)} %bitcast.67), calls=%async_computation.2 | async-start | bytes 131072 | tf_op jit(solution)/shard_map/all_to_all | solution.py:78
  30.5 0.1 all-gather.2.cloned.1.call-done
  30.6 5.1 %fusion.3 = bf16[16,2048]{1,0:T(8,128)(2,1)S(1)} fusion(bf16[1,2048,1792]{2,1,0:T(8,128)(2,1)} %all-gather.2.cloned.1.call-done, bf16[1,1,16,1792]{3,2,1,0:T(8,128)(2,1)} %param.7, f32[16]{0:T(128)S(1)} %fusion.20), kind=kOutput, calls=%fused_computation.8 | convolution fusion | flops 117559296 | bytes 7462976 | tf_op jit(solution)/shard_map/dot_general | solution.py:49
  35.7 0.7 %gather_fusion = bf16[32,2048]{1,0:T(8,128)(2,1)S(1)} fusion(bf16[16,2048]{1,0:T(8,128)(2,1)S(1)} %fusion.3, s32[1024]{0:T(1024)S(1)} %pad_clamp_fusion.2), kind=kCustom, calls=%fused_computation | custom fusion | bytes 262272 | tf_op jit(solution)/shard_map/gather | solution.py:61
  36.4 0.1 reshape.256
  36.4 0.8 %broadcast_select_fusion = bf16[8,4,2048]{2,1,0:T(4,128)(2,1)} fusion(bf16[8,4,2048]{2,1,0:T(4,128)(2,1)S(1)} %reshape.256, pred[8,4]{1,0:T(8,128)(4,1)S(1)} %copy.10), kind=kLoop, calls=%fused_computation.11 | loop fusion | flops 65536 | bytes 262176 | tf_op jit(solution)/shard_map/jit(_where)/select_n | solution.py:60
  37.2 0.0 all-to-all-done.2
  37.2 5.8 %all-to-all-start = ((bf16[8,4,2048]{2,1,0:T(4,128)(2,1)}), bf16[8,4,2048]{2,1,0:T(4,128)(2,1)S(1)}, u32[]{:S(2)}, u32[]{:S(2)}) async-start(bf16[8,4,2048]{2,1,0:T(4,128)(2,1)} %broadcast_select_fusion), calls=%async_computation | async-start | bytes 262144 | tf_op jit(solution)/shard_map/all_to_all | solution.py:63
  43.0 1.9 %all_gather.7 = bf16[32,1792]{1,0:T(8,128)(2,1)S(1)} all-gather(bf16[16,1792]{1,0:T(8,128)(2,1)S(1)} %fusion.8), channel_id=1, replica_groups=mesh['groups'=2,'expert'=4,'dp'=2,'tensor'=2] {'dp'}, dimensions={0}, use_global_device_ids=true | all-gather | bytes 172032 | tf_op jit(solution)/shard_map/all_gather | solution.py:79
  44.9 4.3 %convert_reduce_fusion = bf16[1024,1792]{1,0:T(8,128)(2,1)} fusion(bf16[2,16,1792]{2,1,0:T(8,128)(2,1)S(1)} %bitcast.70, bf16[16,2,1024]{2,0,1:T(8,128)(2,1)S(1)} %all-to-all-done.2), kind=kOutput, calls=%fused_computation.5 | convolution fusion | flops 122945536 | bytes 3850240 | tf_op jit(solution)/shard_map/gcd,gcf->gdf/dot_general | solution.py:82
  49.2 1.3 %all-to-all-done = bf16[8,4,2048]{2,1,0:T(4,128)(2,1)S(1)} async-done(((bf16[8,4,2048]{2,1,0:T(4,128)(2,1)}), bf16[8,4,2048]{2,1,0:T(4,128)(2,1)S(1)}, u32[]{:S(2)}, u32[]{:S(2)}) %all-to-all-start) | async-done | bytes 131104 | tf_op jit(solution)/shard_map/all_to_all | solution.py:63
  50.5 1.1 %fusion.2 = bf16[1,128,2048]{2,1,0:T(8,128)(2,1)} fusion(bf16[32,2048]{1,0:T(8,128)(2,1)S(1)} %reshape.250, s32[32]{0:T(128)S(1)} %eq.100, pred[32]{0:T(512)(128)(4,1)S(1)} %and.91), kind=kOutput, calls=%fused_computation.7 | convolution fusion | flops 17047552 | bytes 655520 | tf_op jit(solution)/shard_map/dot_general | solution.py:74
  (15 shorter events, 0.2 us)
Async XLA Ops:
  7.2 2.6 %copy-start = (bf16[1,128,2048]{2,1,0:T(8,128)(2,1)S(1)}, bf16[1,128,2048]{2,1,0:T(8,128)(2,1)}, u32[]{:S(2)}) copy-start(bf16[1,128,2048]{2,1,0:T(8,128)(2,1)} %param.5) | copy-start | bytes 1572868
  7.2 23.4 %all-gather.2.cloned.1.call-start = ((), (), s32[]{:S(2)}) async-start(), calls=%async_computation.3 | async-start | bytes 11010048 | tf_op jit(solution)/shard_map/all_gather | solution.py:51
  11.3 14.6 %all-to-all-start.1 = ((bf16[8,4,2048]{2,1,0:T(4,128)(2,1)}), bf16[8,4,2048]{2,1,0:T(4,128)(2,1)S(1)}, u32[]{:S(2)}, u32[]{:S(2)}) async-start(bf16[8,4,2048]{2,1,0:T(4,128)(2,1)} %bitcast.10), calls=%async_computation.1 | async-start | bytes 262144 | tf_op jit(solution)/shard_map/all_to_all | solution.py:35
  27.2 10.0 %all-to-all-start.2 = ((bf16[16,2,1024]{2,0,1:T(8,128)(2,1)}), bf16[16,2,1024]{2,0,1:T(8,128)(2,1)S(1)}, u32[]{:S(2)}, u32[]{:S(2)}) async-start(bf16[16,2,1024]{2,0,1:T(8,128)(2,1)} %bitcast.67), calls=%async_computation.2 | async-start | bytes 131072 | tf_op jit(solution)/shard_map/all_to_all | solution.py:78
  37.2 13.3 %all-to-all-start = ((bf16[8,4,2048]{2,1,0:T(4,128)(2,1)}), bf16[8,4,2048]{2,1,0:T(4,128)(2,1)S(1)}, u32[]{:S(2)}, u32[]{:S(2)}) async-start(bf16[8,4,2048]{2,1,0:T(4,128)(2,1)} %broadcast_select_fusion), calls=%async_computation | async-start | bytes 262144 | tf_op jit(solution)/shard_map/all_to_all | solution.py:63
Sparse Core Ops, SparseCore 0:
  9.5 21.0 all-gather.1
where the time goes:
time: 59 us; the launch traced here: 58.4 us
  starting transfers between devices  16.4 us (28%)
  between operations  14.1 us (24%)
  matrix products  10.5 us (18%)
  waiting for transfers between devices  6.92 us (12%)
  local copies, waits for them, and re-layouts  4.56 us (8%)
  other arithmetic  4.02 us (7%)
  blocking collectives  1.88 us (3%)
    all_to_all x1, starting transfers between devices, local(): lax.all_to_all(outgoing_all.reshape(owners, MOST, features), ('expert', '...  7.28 us
    all_to_all x1, starting transfers between devices, local(): lax.all_to_all(returning, ('expert', 'tensor'), split_axis=0, concat_axis...  5.83 us
    dot_general x1, matrix products, local(): lax.dot_general(scaled, lax.all_gather(proj_weight, 'dp', axis=1, tiled=T...  5.11 us
    all_to_all x1, waiting for transfers between devices, local(): lax.all_to_all(outgoing_all.reshape(owners, MOST, features), ('expert', '...  4.91 us
    dot_general x1, matrix products, local(): jnp.einsum('gcd,gcf->gdf', column_share, scaled_all, preferred_element_ty...  4.31 us
    all_to_all x1, starting transfers between devices, local(): lax.all_to_all(slot_rows, 'dp', split_axis=1, concat_axis=0, tiled=True)  3.3 us
    all_gather x1, blocking collectives, local(): scaled_all = lax.all_gather(scaled, 'dp', axis=0, tiled=True)  1.88 us
    all_to_all x1, waiting for transfers between devices, local(): lax.all_to_all(returning, ('expert', 'tensor'), split_axis=0, concat_axis...  1.25 us
  transfers between devices with their start and end apart: 4, of which 3 were waited for; matrix products, arithmetic and copies ran while one was open for 31% of the time, Pallas kernels for 0%

commit v1 on v0

--- a/solution.py
+++ b/solution.py
@@ -32,13 +32,19 @@
     send_row = jnp.sum(jnp.where(selector, local_row[:, None, :], 0), axis=2)
     outgoing = jnp.where(filled[..., None], token_rows[send_row], jnp.zeros((), jnp.bfloat16))
     outgoing_all = jnp.broadcast_to(outgoing[:, None, None], (experts, 2, n_tensor, MOST, features))
-    incoming = lax.all_to_all(
-        outgoing_all.reshape(owners, MOST, features),
-        ("expert", "tensor"),
-        split_axis=0,
-        concat_axis=0,
-        tiled=True,
-    )
+    x = outgoing_all.reshape(owners, MOST, features)
+    ways, here = (lax.axis_size(("expert", "tensor")), lax.axis_index(("expert", "tensor")))
+    width = x.shape[0] // ways
+    shape = list(x.shape)
+    shape[0] = width
+    height = shape[0]
+    shape[0] = height * ways
+    incoming = jnp.zeros(shape, x.dtype)
+    for mask in range(ways):
+        part = lax.dynamic_slice_in_dim(x, (here ^ mask) * width, width, axis=0)
+        if mask:
+            part = lax.ppermute(part, ("expert", "tensor"), [(d, d ^ mask) for d in range(ways)])
+        incoming = lax.dynamic_update_slice_in_dim(incoming, part, (here ^ mask) * height, axis=0)
     incoming = incoming.reshape(owners * MOST, features)
     own_index = own_expert // 2
     own_owners = lax.dynamic_index_in_dim(owner_of, own_index, 0, keepdims=False)

time: 59 us -> 63.2 us (1.071)
  starting transfers between devices: 16.4 us -> 19.3 us
  waiting for transfers between devices: 6.92 us -> 8.51 us
    ppermute x0 -> x7, starting transfers between devices: none -> 12.6 us  [local(): lax.ppermute(part, ('expert', 'tensor'), [(d, d ^ mask) for d in range(wa...]
    all_to_all x1 -> x0, starting transfers between devices: 7.28 us -> none  [local(): lax.all_to_all(outgoing_all.reshape(owners, MOST, features), ('expert', '...]
    ppermute x0 -> x7, waiting for transfers between devices: none -> 6.29 us  [local(): lax.ppermute(part, ('expert', 'tensor'), [(d, d ^ mask) for d in range(wa...]
    all_to_all x1 -> x0, waiting for transfers between devices: 4.91 us -> none  [local(): lax.all_to_all(outgoing_all.reshape(owners, MOST, features), ('expert', '...]
    all_to_all x1, starting transfers between devices: 5.83 us -> 3.37 us  [local(): lax.all_to_all(returning, ('expert', 'tensor'), split_axis=0, concat_axis...]
    broadcast_in_dim x1, local copies, waits for them, and re-layouts: 0.69 us -> 0.04 us  [local(): jnp.broadcast_to(outgoing[:, None, None], (experts, 2, n_tensor, MOST, fe...]
  transfers between devices with their start and end apart: 4 -> 10, of which waited for: 3 -> 3; matrix products, arithmetic and copies ran while one was open for 31% -> 28% of each run, Pallas kernels for 0% -> 0%
where the time goes in v1:
time: 63.2 us; the launch traced here: 62.8 us
  starting transfers between devices  19.3 us (31%)
  between operations  14.3 us (23%)
  matrix products  10.5 us (17%)
  waiting for transfers between devices  8.51 us (13%)
  local copies, waits for them, and re-layouts  4.14 us (7%)
  other arithmetic  4.02 us (6%)
  blocking collectives  2 us (3%)
    ppermute x7, starting transfers between devices, local(): lax.ppermute(part, ('expert', 'tensor'), [(d, d ^ mask) for d in range(wa...  12.6 us
    ppermute x7, waiting for transfers between devices, local(): lax.ppermute(part, ('expert', 'tensor'), [(d, d ^ mask) for d in range(wa...  6.29 us
    dot_general x1, matrix products, local(): lax.dot_general(scaled, lax.all_gather(proj_weight, 'dp', axis=1, tiled=T...  5.11 us
    dot_general x1, matrix products, local(): jnp.einsum('gcd,gcf->gdf', column_share, scaled_all, preferred_element_ty...  4.3 us
    all_to_all x1, starting transfers between devices, local(): lax.all_to_all(returning, ('expert', 'tensor'), split_axis=0, concat_axis...  3.37 us
    all_to_all x1, starting transfers between devices, local(): lax.all_to_all(slot_rows, 'dp', split_axis=1, concat_axis=0, tiled=True)  3.3 us
    all_gather x1, blocking collectives, local(): scaled_all = lax.all_gather(scaled, 'dp', axis=0, tiled=True)  2 us
    all_to_all x1, waiting for transfers between devices, local(): lax.all_to_all(returning, ('expert', 'tensor'), split_axis=0, concat_axis...  1.52 us
  transfers between devices with their start and end apart: 10, of which 3 were waited for; matrix products, arithmetic and copies ran while one was open for 28% of the time, Pallas kernels for 0%

profile of v1, /device:TPU:0, one launch (start us, length us, event | category | flops | bytes accessed | tf_op | source)
XLA Modules:
  0.0 62.8 jit_solution(2255664588654685373)
XLA Ops:
  7.2 0.0 copy-start
  7.2 0.0 all-gather.2.cloned.1.call-start
  7.2 0.7 %all-gather.2.cloned.1.call-update = ((bf16[1,1024,1792]{2,1,0:T(8,128)(2,1)}), bf16[1,2048,1792]{2,1,0:T(8,128)(2,1)}) async-update(((), (), s32[]{:S(2)}) %all-gather.2.cloned.1.call-start, bf16[1,1024,1792]{2,1,0:T(8,128)(2,1)} %param.6) | async-update | bytes 14680088
  8.0 0.7 %broadcast_compare_fusion = (pred[2,16]{1,0:T(4,128)(4,1)S(1)}, s32[2,16]{1,0:T(2,128)S(1)}) fusion(s32[]{:T(128)S(6)} %add.112, s32[1,2,16]{2,1,0:T(2,128)} %param.9), kind=kLoop, calls=%fused_computation.68 | loop fusion | flops 512 | bytes 292 | tf_op jit(solution)/shard_map/eq | solution.py:29
  8.7 0.2 convert_reduce_fusion.1
  8.8 0.7 %and_select_fusion.1 = s32[2,16]{1,0:T(2,128)S(1)} fusion(s32[1,2,16]{2,1,0:T(2,128)} %param.9), kind=kLoop, calls=%fused_computation.59 | loop fusion | flops 352 | bytes 256 | tf_op jit(solution)/shard_map/jit(remainder)/select_n | solution.py:23
  9.5 0.1 select_reduce_fusion
  9.7 0.1 reshape.265
  9.8 0.0 copy-done
  9.8 0.6 gather_fusion.1
  10.4 0.2 fusion.19
  10.6 0.1 broadcast_select_fusion.1
  10.8 0.1 constant_dynamic-slice_fusion
  10.8 3.0 %collective-permute-start = (bf16[1,4,2048]{2,1,0:T(4,128)(2,1)S(1)}, bf16[1,4,2048]{2,1,0:T(4,128)(2,1)S(1)}, u32[]{:S(2)}, u32[]{:S(2)}) collective-permute-start(bf16[1,4,2048]{2,1,0:T(4,128)(2,1)S(1)} %get-tuple-element.10), channel_id=1, source_target_pairs={{0,1},{1,0},{4,5},{5,4},{8,9},{9,8},{12,13},{13,12},{2,3},{3,2},{6... | collective-permute-start | bytes 49160 | tf_op jit(solution)/shard_map/ppermute | solution.py:46
  13.9 1.6 %collective-permute-start.1 = (bf16[1,4,2048]{2,1,0:T(4,128)(2,1)S(1)}, bf16[1,4,2048]{2,1,0:T(4,128)(2,1)S(1)}, u32[]{:S(2)}, u32[]{:S(2)}) collective-permute-start(bf16[1,4,2048]{2,1,0:T(4,128)(2,1)S(1)} %get-tuple-element.9), channel_id=1, source_target_pairs={{0,4},{1,5},{4,0},{5,1},{8,12},{9,13},{12,8},{13,9},{2,6},{3,7},{6... | collective-permute-start | bytes 49160 | tf_op jit(solution)/shard_map/ppermute | solution.py:46
  15.5 0.0 collective-permute-start.2
  15.5 3.0 %collective-permute-start.3 = (bf16[1,4,2048]{2,1,0:T(4,128)(2,1)S(1)}, bf16[1,4,2048]{2,1,0:T(4,128)(2,1)S(1)}, u32[]{:S(2)}, u32[]{:S(2)}) collective-permute-start(bf16[1,4,2048]{2,1,0:T(4,128)(2,1)S(1)} %get-tuple-element.7), channel_id=1, source_target_pairs={{0,8},{1,9},{4,12},{5,13},{8,0},{9,1},{12,4},{13,5},{2,10},{3,11},... | collective-permute-start | bytes 49160 | tf_op jit(solution)/shard_map/ppermute | solution.py:46
  18.5 1.3 %collective-permute-start.4 = (bf16[1,4,2048]{2,1,0:T(4,128)(2,1)S(1)}, bf16[1,4,2048]{2,1,0:T(4,128)(2,1)S(1)}, u32[]{:S(2)}, u32[]{:S(2)}) collective-permute-start(bf16[1,4,2048]{2,1,0:T(4,128)(2,1)S(1)} %get-tuple-element.6), channel_id=1, source_target_pairs={{0,9},{1,8},{4,13},{5,12},{8,1},{9,0},{12,5},{13,4},{2,11},{3,10},... | collective-permute-start | bytes 49160 | tf_op jit(solution)/shard_map/ppermute | solution.py:46
  19.8 0.1 fusion.17
  19.9 0.1 copy.11
  20.0 0.1 reshape.257
  20.1 0.7 %fusion.21 = f32[16]{0:T(128)S(1)} fusion(f32[1,2,16]{2,1,0:T(2,128)} %param.8, s32[]{:T(128)S(6)} %select_n.124), kind=kLoop, calls=%fused_computation.67 | loop fusion | bytes 132 | tf_op jit(solution)/shard_map/jit(dynamic_index_in_dim)/dynamic_slice | solution.py:53
  20.8 0.2 and_reduce_fusion
  21.0 0.9 %fusion.8 = bf16[16,1792]{1,0:T(8,128)(2,1)S(1)} fusion(bf16[1,1,16,1792]{3,2,1,0:T(8,128)(2,1)} %param.7, f32[16]{0:T(128)S(1)} %fusion.21), kind=kLoop, calls=%fused_computation.14 | loop fusion | flops 86016 | bytes 114752 | tf_op jit(solution)/shard_map/convert_element_type | solution.py:54
  21.9 0.1 copy.10
  22.0 0.1 eq.100
  22.1 0.1 and.91
  22.2 0.0 collective-permute-done
  22.2 3.7 %collective-permute-start.5 = (bf16[1,4,2048]{2,1,0:T(4,128)(2,1)S(1)}, bf16[1,4,2048]{2,1,0:T(4,128)(2,1)S(1)}, u32[]{:S(2)}, u32[]{:S(2)}) collective-permute-start(bf16[1,4,2048]{2,1,0:T(4,128)(2,1)S(1)} %get-tuple-element.5), channel_id=1, source_target_pairs={{0,12},{1,13},{4,8},{5,9},{8,4},{9,5},{12,0},{13,1},{2,14},{3,15},... | collective-permute-start | bytes 49160 | tf_op jit(solution)/shard_map/ppermute | solution.py:46
  25.8 0.0 collective-permute-done.1
  25.9 0.1 collective-permute-start.6
  26.0 0.0 collective-permute-done.2
  26.0 0.0 collective-permute-done.3
  26.0 0.0 collective-permute-done.4
  26.1 1.7 %collective-permute-done.5 = bf16[1,4,2048]{2,1,0:T(4,128)(2,1)S(1)} collective-permute-done((bf16[1,4,2048]{2,1,0:T(4,128)(2,1)S(1)}, bf16[1,4,2048]{2,1,0:T(4,128)(2,1)S(1)}, u32[]{:S(2)}, u32[]{:S(2)}) %collective-permute-start.5) | collective-permute-done | bytes 16416 | tf_op jit(solution)/shard_map/ppermute | solution.py:46
  27.8 4.6 %collective-permute-done.6 = bf16[1,4,2048]{2,1,0:T(4,128)(2,1)S(1)} collective-permute-done((bf16[1,4,2048]{2,1,0:T(4,128)(2,1)S(1)}, bf16[1,4,2048]{2,1,0:T(4,128)(2,1)S(1)}, u32[]{:S(2)}, u32[]{:S(2)}) %collective-permute-start.6) | collective-permute-done | bytes 16416 | tf_op jit(solution)/shard_map/ppermute | solution.py:46
  32.4 0.6 gather_fusion.2
  33.0 0.6 %copy.15 = bf16[2,2,8,1024]{3,2,0,1:T(8,128)(2,1)} copy(bf16[2,2,8,1024]{3,2,1,0:T(8,128)(2,1)S(1)} %bitcast.72) | data formatting | bytes 131072 | tf_op jit(solution)/shard_map/all_to_all | solution.py:84
  33.7 3.3 %all-to-all-start.1 = ((bf16[16,2,1024]{2,0,1:T(8,128)(2,1)}), bf16[16,2,1024]{2,0,1:T(8,128)(2,1)S(1)}, u32[]{:S(2)}, u32[]{:S(2)}) async-start(bf16[16,2,1024]{2,0,1:T(8,128)(2,1)} %bitcast.67), calls=%async_computation.1 | async-start | bytes 131072 | tf_op jit(solution)/shard_map/all_to_all | solution.py:84
  37.0 0.0 all-gather.2.cloned.1.call-done
  37.0 5.1 %fusion.3 = bf16[16,2048]{1,0:T(8,128)(2,1)S(1)} fusion(bf16[1,2048,1792]{2,1,0:T(8,128)(2,1)} %all-gather.2.cloned.1.call-done, bf16[1,1,16,1792]{3,2,1,0:T(8,128)(2,1)} %param.7, f32[16]{0:T(128)S(1)} %fusion.21), kind=kOutput, calls=%fused_computation.8 | convolution fusion | flops 117559296 | bytes 7462976 | tf_op jit(solution)/shard_map/dot_general | solution.py:55
  42.1 0.7 %gather_fusion = bf16[32,2048]{1,0:T(8,128)(2,1)S(1)} fusion(bf16[16,2048]{1,0:T(8,128)(2,1)S(1)} %fusion.3, s32[1024]{0:T(1024)S(1)} %pad_clamp_fusion.2), kind=kCustom, calls=%fused_computation | custom fusion | bytes 262272 | tf_op jit(solution)/shard_map/gather | solution.py:67
  42.8 0.1 reshape.256
  42.8 0.8 %broadcast_select_fusion = bf16[8,4,2048]{2,1,0:T(4,128)(2,1)} fusion(bf16[8,4,2048]{2,1,0:T(4,128)(2,1)S(1)} %reshape.256, pred[8,4]{1,0:T(8,128)(4,1)S(1)} %copy.10), kind=kLoop, calls=%fused_computation.11 | loop fusion | flops 65536 | bytes 262176 | tf_op jit(solution)/shard_map/jit(_where)/select_n | solution.py:66
  43.6 0.0 all-to-all-done.1
  43.6 3.4 %all-to-all-start = ((bf16[8,4,2048]{2,1,0:T(4,128)(2,1)}), bf16[8,4,2048]{2,1,0:T(4,128)(2,1)S(1)}, u32[]{:S(2)}, u32[]{:S(2)}) async-start(bf16[8,4,2048]{2,1,0:T(4,128)(2,1)} %broadcast_select_fusion), calls=%async_computation | async-start | bytes 262144 | tf_op jit(solution)/shard_map/all_to_all | solution.py:69
  47.0 2.0 %all_gather.7 = bf16[32,1792]{1,0:T(8,128)(2,1)S(1)} all-gather(bf16[16,1792]{1,0:T(8,128)(2,1)S(1)} %fusion.8), channel_id=1, replica_groups=mesh['groups'=2,'expert'=4,'dp'=2,'tensor'=2] {'dp'}, dimensions={0}, use_global_device_ids=true | all-gather | bytes 172032 | tf_op jit(solution)/shard_map/all_gather | solution.py:85
  49.0 4.3 %convert_reduce_fusion = bf16[1024,1792]{1,0:T(8,128)(2,1)} fusion(bf16[2,16,1792]{2,1,0:T(8,128)(2,1)S(1)} %bitcast.71, bf16[16,2,1024]{2,0,1:T(8,128)(2,1)S(1)} %all-to-all-done.1), kind=kOutput, calls=%fused_computation.5 | convolution fusion | flops 122945536 | bytes 3850240 | tf_op jit(solution)/shard_map/gcd,gcf->gdf/dot_general | solution.py:88
  53.3 1.5 %all-to-all-done = bf16[8,4,2048]{2,1,0:T(4,128)(2,1)S(1)} async-done(((bf16[8,4,2048]{2,1,0:T(4,128)(2,1)}), bf16[8,4,2048]{2,1,0:T(4,128)(2,1)S(1)}, u32[]{:S(2)}, u32[]{:S(2)}) %all-to-all-start) | async-done | bytes 131104 | tf_op jit(solution)/shard_map/all_to_all | solution.py:69
  54.9 1.1 %fusion.2 = bf16[1,128,2048]{2,1,0:T(8,128)(2,1)} fusion(bf16[32,2048]{1,0:T(8,128)(2,1)S(1)} %reshape.250, s32[32]{0:T(128)S(1)} %eq.100, pred[32]{0:T(512)(128)(4,1)S(1)} %and.91), kind=kOutput, calls=%fused_computation.7 | convolution fusion | flops 17047552 | bytes 655520 | tf_op jit(solution)/shard_map/dot_general | solution.py:80
  (24 shorter events, 0.4 us)
Async XLA Ops:
  7.2 2.6 %copy-start = (bf16[1,128,2048]{2,1,0:T(8,128)(2,1)S(1)}, bf16[1,128,2048]{2,1,0:T(8,128)(2,1)}, u32[]{:S(2)}) copy-start(bf16[1,128,2048]{2,1,0:T(8,128)(2,1)} %param.5) | copy-start | bytes 1572868
  7.2 29.8 %all-gather.2.cloned.1.call-start = ((), (), s32[]{:S(2)}) async-start(), calls=%async_computation.2 | async-start | bytes 11010048 | tf_op jit(solution)/shard_map/all_gather | solution.py:57
  10.8 11.3 %collective-permute-start = (bf16[1,4,2048]{2,1,0:T(4,128)(2,1)S(1)}, bf16[1,4,2048]{2,1,0:T(4,128)(2,1)S(1)}, u32[]{:S(2)}, u32[]{:S(2)}) collective-permute-start(bf16[1,4,2048]{2,1,0:T(4,128)(2,1)S(1)} %get-tuple-element.10), channel_id=1, source_target_pairs={{0,1},{1,0},{4,5},{5,4},{8,9},{9,8},{12,13},{13,12},{2,3},{3,2},{6... | collective-permute-start | bytes 49160 | tf_op jit(solution)/shard_map/ppermute | solution.py:46
  13.9 12.0 %collective-permute-start.1 = (bf16[1,4,2048]{2,1,0:T(4,128)(2,1)S(1)}, bf16[1,4,2048]{2,1,0:T(4,128)(2,1)S(1)}, u32[]{:S(2)}, u32[]{:S(2)}) collective-permute-start(bf16[1,4,2048]{2,1,0:T(4,128)(2,1)S(1)} %get-tuple-element.9), channel_id=1, source_target_pairs={{0,4},{1,5},{4,0},{5,1},{8,12},{9,13},{12,8},{13,9},{2,6},{3,7},{6... | collective-permute-start | bytes 49160 | tf_op jit(solution)/shard_map/ppermute | solution.py:46
  15.5 10.5 %collective-permute-start.2 = (bf16[1,4,2048]{2,1,0:T(4,128)(2,1)S(1)}, bf16[1,4,2048]{2,1,0:T(4,128)(2,1)S(1)}, u32[]{:S(2)}, u32[]{:S(2)}) collective-permute-start(bf16[1,4,2048]{2,1,0:T(4,128)(2,1)S(1)} %get-tuple-element.8), channel_id=1, source_target_pairs={{0,5},{1,4},{4,1},{5,0},{8,13},{9,12},{12,9},{13,8},{2,7},{3,6},{6... | collective-permute-start | bytes 49160 | tf_op jit(solution)/shard_map/ppermute | solution.py:46
  15.5 10.5 %collective-permute-start.3 = (bf16[1,4,2048]{2,1,0:T(4,128)(2,1)S(1)}, bf16[1,4,2048]{2,1,0:T(4,128)(2,1)S(1)}, u32[]{:S(2)}, u32[]{:S(2)}) collective-permute-start(bf16[1,4,2048]{2,1,0:T(4,128)(2,1)S(1)} %get-tuple-element.7), channel_id=1, source_target_pairs={{0,8},{1,9},{4,12},{5,13},{8,0},{9,1},{12,4},{13,5},{2,10},{3,11},... | collective-permute-start | bytes 49160 | tf_op jit(solution)/shard_map/ppermute | solution.py:46
  18.5 7.6 %collective-permute-start.4 = (bf16[1,4,2048]{2,1,0:T(4,128)(2,1)S(1)}, bf16[1,4,2048]{2,1,0:T(4,128)(2,1)S(1)}, u32[]{:S(2)}, u32[]{:S(2)}) collective-permute-start(bf16[1,4,2048]{2,1,0:T(4,128)(2,1)S(1)} %get-tuple-element.6), channel_id=1, source_target_pairs={{0,9},{1,8},{4,13},{5,12},{8,1},{9,0},{12,5},{13,4},{2,11},{3,10},... | collective-permute-start | bytes 49160 | tf_op jit(solution)/shard_map/ppermute | solution.py:46
  22.2 5.6 %collective-permute-start.5 = (bf16[1,4,2048]{2,1,0:T(4,128)(2,1)S(1)}, bf16[1,4,2048]{2,1,0:T(4,128)(2,1)S(1)}, u32[]{:S(2)}, u32[]{:S(2)}) collective-permute-start(bf16[1,4,2048]{2,1,0:T(4,128)(2,1)S(1)} %get-tuple-element.5), channel_id=1, source_target_pairs={{0,12},{1,13},{4,8},{5,9},{8,4},{9,5},{12,0},{13,1},{2,14},{3,15},... | collective-permute-start | bytes 49160 | tf_op jit(solution)/shard_map/ppermute | solution.py:46
  25.9 6.5 %collective-permute-start.6 = (bf16[1,4,2048]{2,1,0:T(4,128)(2,1)S(1)}, bf16[1,4,2048]{2,1,0:T(4,128)(2,1)S(1)}, u32[]{:S(2)}, u32[]{:S(2)}) collective-permute-start(bf16[1,4,2048]{2,1,0:T(4,128)(2,1)S(1)} %get-tuple-element.4), channel_id=1, source_target_pairs={{0,13},{1,12},{4,9},{5,8},{8,5},{9,4},{12,1},{13,0},{2,15},{3,14},... | collective-permute-start | bytes 49160 | tf_op jit(solution)/shard_map/ppermute | solution.py:46
  33.7 10.0 %all-to-all-start.1 = ((bf16[16,2,1024]{2,0,1:T(8,128)(2,1)}), bf16[16,2,1024]{2,0,1:T(8,128)(2,1)S(1)}, u32[]{:S(2)}, u32[]{:S(2)}) async-start(bf16[16,2,1024]{2,0,1:T(8,128)(2,1)} %bitcast.67), calls=%async_computation.1 | async-start | bytes 131072 | tf_op jit(solution)/shard_map/all_to_all | solution.py:84
  43.6 11.2 %all-to-all-start = ((bf16[8,4,2048]{2,1,0:T(4,128)(2,1)}), bf16[8,4,2048]{2,1,0:T(4,128)(2,1)S(1)}, u32[]{:S(2)}, u32[]{:S(2)}) async-start(bf16[8,4,2048]{2,1,0:T(4,128)(2,1)} %broadcast_select_fusion), calls=%async_computation | async-start | bytes 262144 | tf_op jit(solution)/shard_map/all_to_all | solution.py:69
Sparse Core Ops, SparseCore 0:
  9.5 21.0 all-gather.1
